TPU v7x, 128 devices: a whole 4x4x4 slice. The times are simulated.
128 devices in a mesh: dp: 64 (over y, x, z), rep: 2 (over core).
Axes of the slice: x: 4, y: 4, z: 4, core: 2. Of those that a mesh axis runs over, the one named last changes fastest.
Arguments:
- row_grads: float32 [65536, 512], P(('dp', 'rep')), may hold values from -2500 to 2500
- token_owner: int32 [65536, 1], P(('dp', 'rep')), may hold values from 0 to 63; in each aligned block of 512 rows (0 to 511, 512 to 1023, ...) at most 16 rows name the same one
- token_row: int32 [65536], P(('dp', 'rep')), may hold values from 0 to 2047
- table: float32 [131072, 512], P('dp'), may hold values from -6 to 6
- moment: float32 [131072, 512], P('dp'), may hold values from -3 to 3
- second: float32 [131072, 512], P('dp'), may hold values from 0.05 to 2
Outputs:
- new_table: float32 [131072, 512], P('dp')
- new_moment: float32 [131072, 512], P('dp')
- new_second: float32 [131072, 512], P('dp')
Inputs may be any that keep to these rules, and one draw needn't show every extreme that they name: `token_owner`: among the rows of one device at most 16 name one owner; in every draw some owner is named by exactly 16 rows of some device.
All inputs are finite; a program needn't handle non-finite values.
Results may differ from a plain program's by a relative error of at most 0.00007.
Values sent between devices are 32-bit elements; how exact they have to be, the bound alone decides.
No kernel may reach another device: no remote copies, remote signals or barrier semaphores. Data moves between devices by JAX's collectives and lax.ppermute only.
A program may use at most 128 MiB of HBM per device.

v0:
```python
import jax
import jax.numpy as jnp
from jax import lax
from jax.sharding import PartitionSpec as P

VOCAB = 131072
ADAM_STEP = 100
LW = 512


def copy_for_each(value, axis):
    size = lax.axis_size(axis)
    return lax.all_to_all(
        jnp.broadcast_to(value[None], (size, *value.shape)), axis, 0, 0, tiled=True
    )


def of_everyone(value, axis):
    return copy_for_each(value, axis).sum(axis=0)


def accumulate(row_ids, sent_rows, row_start, row_count):
    local_ids = row_ids - row_start
    feature_cols = sent_rows.shape[1]
    inside = (local_ids >= 0) & (local_ids < row_count)
    slot_index = jnp.where(inside, local_ids, row_count)
    return (
        jnp.zeros((row_count, feature_cols), jnp.float32).at[slot_index].add(sent_rows, mode="drop")
    )


def adamw(table_rows, moment_rows, second_rows, dense_grad, scaling):
    clipped = scaling * dense_grad
    new_moment = 0.9 * moment_rows + 0.1 * clipped
    new_second = 0.999 * second_rows + 0.001 * clipped * clipped
    first_fix = 1.0 - 0.9**ADAM_STEP
    second_fix = 1.0 - 0.999**ADAM_STEP
    update = new_moment / first_fix / (jnp.sqrt(new_second / second_fix) + 1e-08)
    new_table = table_rows - 0.01 * (update + 0.01 * table_rows)
    return (new_table, new_moment, new_second)


def clip_factor(total):
    limit = 0.5 * jnp.sqrt(jnp.float32(VOCAB * LW))
    return jnp.minimum(jnp.float32(1.0), limit / (jnp.sqrt(total) + 1e-06))


def local(row_grads, token_owner, token_row, table, moment, second):
    owners = lax.axis_size("dp")
    tokens_here = row_grads.shape[0]
    feature_cols = row_grads.shape[1]
    rows_owned = table.shape[0]
    capacity = 2 * tokens_here // owners
    owner_ids = token_owner[:, 0]
    owner_hits = (owner_ids[:, None] == jnp.arange(owners, dtype=jnp.int32)[None, :]).astype(
        jnp.int32
    )
    earlier = jnp.cumsum(owner_hits, axis=0) - owner_hits
    position = jnp.sum(earlier * owner_hits, axis=1)
    destination = owner_ids * capacity + position
    send_rows = (
        jnp.zeros((owners * capacity, feature_cols), jnp.float32).at[destination].set(row_grads)
    )
    send_ids = jnp.zeros((owners * capacity,), jnp.int32).at[destination].set(token_row)
    received, received_ids = (
        lax.all_to_all(
            send_rows.reshape(owners, capacity, feature_cols),
            "dp",
            split_axis=0,
            concat_axis=0,
            tiled=True,
        ),
        lax.all_to_all(
            send_ids.reshape(owners, capacity), "dp", split_axis=0, concat_axis=0, tiled=True
        ),
    )
    flat_rows = received.reshape(owners * capacity, feature_cols)
    flat_ids = received_ids.reshape(owners * capacity)
    dense = of_everyone(accumulate(flat_ids, flat_rows, 0, rows_owned), "rep")
    total = of_everyone(jnp.sum(dense * dense), "dp")
    scaling = clip_factor(total)
    new_table, new_moment, new_second = adamw(table, moment, second, dense, scaling)
    return (new_table, new_moment, new_second)


def solution(mesh):
    return jax.shard_map(
        local,
        mesh=mesh,
        in_specs=(
            P(("dp", "rep"), None),
            P(("dp", "rep"), None),
            P(("dp", "rep")),
            P("dp", None),
            P("dp", None),
            P("dp", None),
        ),
        out_specs=(P("dp", None), P("dp", None), P("dp", None)),
        check_vma=False,
    )
```

profile of v0, /device:TPU:1, one launch (start us, length us, event | category | flops | bytes accessed | tf_op | source)
XLA Modules:
  0.0 125.1 jit_solution(15020301319457739451)
XLA Ops:
  0.6 0.7 fusion.8
  1.3 1.2 reduce-window.6
  2.5 0.2 slice_reduce_fusion
  2.8 0.8 fusion.7
  3.6 0.7 compare_select_fusion.1
  4.3 2.6 %scatter_custom_fusion = s32[1024]{0:T(1024)S(1)} fusion(s32[512]{0:T(512)S(1)} %bitcast.34, s32[512]{0:T(512)} %param.8, s32[]{:T(128)} %constant.19.clone.1), kind=kCustom, calls=%fused_computation.24 | custom fusion | bytes 4608 | tf_op jit(solution)/shard_map/scatter | solution.py:64
  6.9 0.7 all_to_all.16
  7.6 12.0 %all-to-all-start = ((s32[64,1,16]{2,1,0:T(1,128)}), s32[64,1,16]{2,1,0:T(1,128)S(1)}, u32[]{:S(2)}, u32[]{:S(2)}) async-start(s32[64,1,16]{2,1,0:T(1,128)} %bitcast.5), calls=%async_computation | async-start | bytes 65536 | tf_op jit(solution)/shard_map/all_to_all | solution.py:73
  19.6 4.3 %scatter_custom_fusion.1 = f32[1024,512]{1,0:T(8,128)} fusion(s32[512]{0:T(512)S(1)} %bitcast.35, f32[512,512]{1,0:T(8,128)} %param.6, f32[]{:T(128)} %constant.18.clone.1), kind=kCustom, calls=%fused_computation.10 | custom fusion | bytes 2097664 | tf_op jit(solution)/shard_map/scatter | solution.py:62
  23.9 4.0 %all-to-all-done = s32[64,1,16]{2,1,0:T(1,128)S(1)} async-done(((s32[64,1,16]{2,1,0:T(1,128)}), s32[64,1,16]{2,1,0:T(1,128)S(1)}, u32[]{:S(2)}, u32[]{:S(2)}) %all-to-all-start) | async-done | bytes 4128 | tf_op jit(solution)/shard_map/all_to_all | solution.py:73
  27.9 5.7 %all-to-all-start.1 = ((f32[64,16,512]{2,1,0:T(8,128)}), f32[64,16,512]{2,1,0:T(8,128)S(1)}, u32[]{:S(2)}, u32[]{:S(2)}) async-start(f32[64,16,512]{2,1,0:T(8,128)} %bitcast.7), calls=%async_computation.1 | async-start | bytes 4194304 | tf_op jit(solution)/shard_map/all_to_all | solution.py:66
  33.7 0.5 broadcast.95
  34.2 0.7 reduce.6
  34.9 0.1 reshape.82
  35.0 25.9 %all-to-all-done.1 = f32[64,16,512]{2,1,0:T(8,128)S(1)} async-done(((f32[64,16,512]{2,1,0:T(8,128)}), f32[64,16,512]{2,1,0:T(8,128)S(1)}, u32[]{:S(2)}, u32[]{:S(2)}) %all-to-all-start.1) | async-done | bytes 2097184 | tf_op jit(solution)/shard_map/all_to_all | solution.py:66
  60.9 9.0 %scatter_custom_fusion.2 = f32[2048,512]{1,0:T(8,128)} fusion(s32[1024]{0:T(1024)S(1)} %bitcast.33, f32[1024,512]{1,0:T(8,128)S(1)} %bitcast.29, f32[]{:T(128)} %constant.18.clone.1), kind=kCustom, calls=%fused_computation.8 | custom fusion | flops 524288 | bytes 4194308 | tf_op jit(solution)/shard_map/scatter-add | solution.py:28
  69.8 3.4 %broadcast_in_dim.12 = f32[2,2048,512]{2,1,0:T(8,128)S(1)} broadcast(f32[2048,512]{1,0:T(8,128)} %scatter_custom_fusion.2), dimensions={1,2} | broadcast | bytes 12582912 | tf_op jit(solution)/shard_map/broadcast_in_dim | solution.py:14
  73.2 14.8 %all_to_all.25 = f32[2,2048,512]{2,1,0:T(8,128)} all-to-all(f32[2,2048,512]{2,1,0:T(8,128)S(1)} %broadcast_in_dim.12), channel_id=1, replica_groups=mesh['dp'=64,'rep'=2] {'rep'}, dimensions={0} | all-to-all | bytes 16777216 | tf_op jit(solution)/shard_map/all_to_all | solution.py:13
  88.0 6.8 %reduce_sum.40 = f32[2048,512]{1,0:T(8,128)} reduce(f32[2,2048,512]{2,1,0:T(8,128)} %all_to_all.25, f32[]{:T(128)} %constant.18.clone.1), dimensions={0}, to_apply=%region_6.7 | reduce | flops 1048576 | bytes 12582916 | tf_op jit(solution)/shard_map/reduce_sum | solution.py:19
  94.8 3.9 %multiply_reduce_fusion = f32[]{:T(128)} fusion(f32[2048,512]{1,0:T(8,128)} %reduce_sum.40), kind=kLoop, calls=%fused_computation.7 | loop fusion | flops 2097151 | bytes 4194308 | tf_op jit(solution)/shard_map/reduce_sum | solution.py:80
  98.7 0.7 broadcast_in_dim.13
  99.4 13.2 %all_to_all.26 = f32[64,1,1]{2,1,0:T(1,128)S(1)} all-to-all(f32[64,1,1]{2,1,0:T(1,128)S(1)} %broadcast_in_dim.13), channel_id=1, replica_groups=mesh['dp'=64,'rep'=2] {'dp'}, dimensions={0} | all-to-all | bytes 512 | tf_op jit(solution)/shard_map/all_to_all | solution.py:13
  112.5 0.7 reduce_sum.42
  113.9 11.2 %multiply_subtract_fusion = (f32[2048,512]{1,0:T(8,128)}, f32[2048,512]{1,0:T(8,128)}, f32[2048,512]{1,0:T(8,128)}) fusion(f32[2048,512]{1,0:T(8,128)} %param.9, f32[2048,512]{1,0:T(8,128)} %reduce_sum.40, f32[]{:T(128)S(6)} %min_shard_map.3, f32[2048,512]{1,0:T(8,128)} %param.10, f32[2048,512]{1,0:T(8,128)} %param.11), kind=kLoop, calls=%fused_computation.5 | loop fusion | flops 16777216 | bytes 29360132 | tf_op jit(solution)/shard_map/sub | solution.py:39
  (3 shorter events, 0.1 us)
Async XLA Ops:
  7.6 20.3 %all-to-all-start = ((s32[64,1,16]{2,1,0:T(1,128)}), s32[64,1,16]{2,1,0:T(1,128)S(1)}, u32[]{:S(2)}, u32[]{:S(2)}) async-start(s32[64,1,16]{2,1,0:T(1,128)} %bitcast.5), calls=%async_computation | async-start | bytes 65536 | tf_op jit(solution)/shard_map/all_to_all | solution.py:73
  27.9 33.0 %all-to-all-start.1 = ((f32[64,16,512]{2,1,0:T(8,128)}), f32[64,16,512]{2,1,0:T(8,128)S(1)}, u32[]{:S(2)}, u32[]{:S(2)}) async-start(f32[64,16,512]{2,1,0:T(8,128)} %bitcast.7), calls=%async_computation.1 | async-start | bytes 4194304 | tf_op jit(solution)/shard_map/all_to_all | solution.py:66
where the time goes:
time: 126 us; the launch traced here: 125 us
  other arithmetic  35.6 us (28%)
  waiting for transfers between devices  29.9 us (24%)
  blocking collectives  28 us (22%)
  starting transfers between devices  17.7 us (14%)
  local copies, waits for them, and re-layouts  12.5 us (10%)
  between operations  1.43 us (1%)
    all_to_all x2, blocking collectives, copy_for_each(): lax.all_to_all(jnp.broadcast_to(value[None], (size, *value.shape)), axis,...  28 us
    all_to_all x1, waiting for transfers between devices, local(): lax.all_to_all(send_rows.reshape(owners, capacity, feature_cols), 'dp', s...  25.9 us
    all_to_all x1, starting transfers between devices, local(): lax.all_to_all(send_ids.reshape(owners, capacity), 'dp', split_axis=0, co...  12 us
    sub x1, other arithmetic, adamw(): new_table = table_rows - 0.01 * (update + 0.01 * table_rows)  11.2 us
    scatter-add x1, other arithmetic, accumulate(): jnp.zeros((row_count, feature_cols), jnp.float32).at[slot_index]  8.95 us
    reduce_sum x2, other arithmetic, of_everyone(): return copy_for_each(value, axis).sum(axis=0)  7.48 us
    all_to_all x1, starting transfers between devices, local(): lax.all_to_all(send_rows.reshape(owners, capacity, feature_cols), 'dp', s...  5.75 us
    scatter x1, local copies, waits for them, and re-layouts, local(): jnp.zeros((owners * capacity, feature_cols), jnp.float32).at[destination]  4.32 us
  transfers between devices with their start and end apart: 2, of which 2 were waited for; matrix products, arithmetic and copies ran while one was open for 5% of the time, Pallas kernels for 0%

commit v1 on v0

v1 whole, which is shorter than its diff:
```python
import jax
import jax.numpy as jnp
from jax import lax
from jax.experimental import pallas as pl
from jax.experimental.pallas import tpu as pltpu
from jax.sharding import PartitionSpec as P

VOCAB = 131072
ADAM_STEP = 100
LW = 512
OWNERS = 64
SLOTS = 16
TOKENS = 512
ROWS = 2048
DEVICES = 128
BLOCK = 2 * SLOTS + 1
PITCH = 2064
CHAINS = 4
CHUNK = 128
AXES = ("dp", "rep")
VMEM = pltpu.MemorySpace.VMEM
SMEM = pltpu.MemorySpace.SMEM


def pack_kernel(owner, row, x, send, ids_v, ids_s, sem):
    line = lax.broadcasted_iota(jnp.int32, (16, 128), 0)
    ids_v[...] = jnp.where(line < 8, ROWS, 0)
    copy = pltpu.make_async_copy(ids_v, ids_s, sem)
    copy.start()
    copy.wait()

    def tokens(step, _):
        for k in range(8):
            t = step * 8 + k
            o = owner[t]
            p = ids_s[8, o]
            ids_s[8, o] = p + 1
            ids_s[o >> 3, ((o & 7) << 4) + p] = row[t]
            base = step * 32 + k
            block = o * (2 * BLOCK) + p
            send[pl.ds(block, 2, stride=SLOTS), :] = x[pl.ds(base, 2, stride=8), :]
            send[pl.ds(block + BLOCK, 2, stride=SLOTS), :] = x[pl.ds(base + 16, 2, stride=8), :]
        return 0

    lax.fori_loop(0, TOKENS // 8, tokens, 0)
    copy = pltpu.make_async_copy(ids_s, ids_v, sem)
    copy.start()
    copy.wait()
    ids = ids_v[0:8, :].astype(jnp.float32)
    mine = lax.rem(lax.axis_index("dp") * 2 + lax.axis_index("rep"), 8)
    lane = lax.broadcasted_iota(jnp.int32, (8, 128), 1)
    for b in range(8):
        turned = pltpu.roll(ids, lax.rem((mine - b + 8) * SLOTS, 128), 1)
        line = jnp.where((lane >> 4) == mine, turned, 0.0)
        for h in range(2):
            send[pl.ds((2 * b + h) * BLOCK + 2 * SLOTS, 8, stride=16 * BLOCK), :] = line


def pack(owner, row, x):
    return pl.pallas_call(
        pack_kernel,
        out_shape=jax.ShapeDtypeStruct((DEVICES * BLOCK, 128), jnp.float32),
        in_specs=[
            pl.BlockSpec(memory_space=SMEM),
            pl.BlockSpec(memory_space=SMEM),
            pl.BlockSpec(memory_space=VMEM),
        ],
        out_specs=pl.BlockSpec(memory_space=VMEM),
        scratch_shapes=[
            pltpu.VMEM((16, 128), jnp.int32),
            pltpu.SMEM((16, 128), jnp.int32),
            pltpu.SemaphoreType.DMA,
        ],
        compiler_params=pltpu.CompilerParams(vmem_limit_bytes=8 * 2**20),
        name="pack",
    )(owner, row, x)


def sum_kernel(recv, half, squares, ids_v, ids_s, sem, *sums):
    for g in range(16):
        lines = recv[pl.ds(g * 8 * BLOCK + 2 * SLOTS, 8, stride=BLOCK), :]
        ids_v[g : g + 1, :] = jnp.sum(lines, axis=0, keepdims=True).astype(jnp.int32)
    copy = pltpu.make_async_copy(ids_v, ids_s, sem)
    copy.start()

    def clear(i, _):
        for total in sums:
            for k in range(8):
                total[pl.ds(i * 64 + k * 8, 8), :] = jnp.zeros((8, 128), jnp.float32)
        return 0

    lax.fori_loop(0, 2 * PITCH // 64, clear, 0)
    for total in sums:
        for k in range(2 * PITCH // 64 * 64, 2 * PITCH, 8):
            total[k : k + 8, :] = jnp.zeros((8, 128), jnp.float32)
    copy.wait()
    groups = 16 // CHAINS

    def add(i, _):
        g, s = i // 8, lax.rem(i, 8)
        for p in range(SLOTS):
            for c, total in enumerate(sums):
                r = ids_s[g + c * groups, s * SLOTS + p]
                line = ((g + c * groups) * 8 + s) * BLOCK + p
                spot = pl.ds(r, 2, stride=PITCH)
                total[spot, :] = total[spot, :] + recv[pl.ds(line, 2, stride=SLOTS), :]
        return 0

    lax.fori_loop(0, groups * 8, add, 0)

    def fold(i, squared):
        squared = list(squared)
        for k in range(4):
            for j in range(2):
                at = pl.multiple_of(j * PITCH + i * 32 + k * 8, 8)
                parts = [total[pl.ds(at, 8), :] for total in sums]
                while len(parts) > 1:
                    parts = [a + b for a, b in zip(parts[::2], parts[1::2])]
                half[pl.ds(pl.multiple_of(i * 32 + k * 8, 8), 8), j * 128 : (j + 1) * 128] = parts[0]
                squared[k] = squared[k] + parts[0] * parts[0]
        return tuple(squared)

    zero = jnp.zeros((8, 128), jnp.float32)
    a, b, c, d = lax.fori_loop(0, ROWS // 32, fold, (zero,) * 4)
    squares[...] = jnp.broadcast_to(jnp.sum((a + b) + (c + d), axis=0, keepdims=True), squares.shape)


def sum_rows(recv):
    return pl.pallas_call(
        sum_kernel,
        out_shape=(
            jax.ShapeDtypeStruct((ROWS, 256), jnp.float32),
            jax.ShapeDtypeStruct((DEVICES, 128), jnp.float32),
        ),
        in_specs=[pl.BlockSpec(memory_space=VMEM)],
        out_specs=(pl.BlockSpec(memory_space=VMEM), pl.BlockSpec(memory_space=VMEM)),
        scratch_shapes=[
            pltpu.VMEM((16, 128), jnp.int32),
            pltpu.SMEM((16, 128), jnp.int32),
            pltpu.SemaphoreType.DMA,
        ]
        + [pltpu.VMEM((2 * PITCH, 128), jnp.float32)] * CHAINS,
        compiler_params=pltpu.CompilerParams(vmem_limit_bytes=18 * 2**20),
        name="sum_rows",
    )(recv)


def update_kernel(part, own, other, table, moment, second, *rest):
    outs, bufs, sems = rest[0:3], rest[3:6], rest[6]
    total = jnp.sum(part[...], keepdims=True)
    limit = 0.5 * float(VOCAB * LW) ** 0.5
    clip = jnp.minimum(1.0, limit / (jnp.sqrt(total) + 1e-06))
    scale = jnp.broadcast_to(clip, (8, 128))
    first_fix = 1.0 - 0.9**ADAM_STEP
    second_fix = 1.0 - 0.999**ADAM_STEP
    rep = lax.axis_index("rep")
    new_table, new_moment, new_second = bufs

    def tile(i, _):
        for k in range(2):
            rows = pl.ds(pl.multiple_of(i * 16 + k * 8, 8), 8)
            for h, source in enumerate((own, other)):
                start = jnp.where(rep == 0, h, 1 - h) * 256
                for j in range(2):
                    cols = pl.ds(pl.multiple_of(start + j * 128, 128), 128)
                    g = scale * source[rows, j * 128 : (j + 1) * 128]
                    nm = 0.9 * moment[rows, cols] + 0.1 * g
                    nv = 0.999 * second[rows, cols] + 0.001 * g * g
                    root = jnp.sqrt(nv * (1.0 / second_fix)) + 1e-08
                    t = table[rows, cols]
                    new_moment[rows, cols] = nm
                    new_second[rows, cols] = nv
                    new_table[rows, cols] = t - 0.01 * ((nm * (1.0 / first_fix)) / root + 0.01 * t)
        return 0

    def copies(c):
        rows = pl.ds(pl.multiple_of(c * CHUNK, CHUNK), CHUNK)
        return [
            pltpu.make_async_copy(buf.at[rows], out.at[rows], sems.at[n, c])
            for n, (buf, out) in enumerate(zip(bufs, outs))
        ]

    steps = CHUNK // 16
    for c in range(ROWS // CHUNK):
        lax.fori_loop(c * steps, (c + 1) * steps, tile, 0)
        for copy in copies(c):
            copy.start()
    for c in range(ROWS // CHUNK):
        for copy in copies(c):
            copy.wait()


def update(part, own, other, table, moment, second):
    shape = jax.ShapeDtypeStruct((ROWS, LW), jnp.float32)
    return pl.pallas_call(
        update_kernel,
        out_shape=(shape,) * 3,
        in_specs=[pl.BlockSpec(memory_space=VMEM)] * 6,
        out_specs=(pl.BlockSpec(memory_space=pl.ANY),) * 3,
        scratch_shapes=[pltpu.VMEM((ROWS, LW), jnp.float32)] * 3
        + [pltpu.SemaphoreType.DMA((3, ROWS // CHUNK))],
        compiler_params=pltpu.CompilerParams(vmem_limit_bytes=34 * 2**20),
        name="update",
    )(part, own, other, table, moment, second)


def local(row_grads, token_owner, token_row, table, moment, second):
    x = row_grads.reshape(64, 8, 4, 128).transpose(0, 2, 1, 3).reshape(4 * TOKENS, 128)
    send = pack(token_owner[:, 0], token_row, x)
    recv = lax.all_to_all(send.reshape(DEVICES, 1, BLOCK * 128), AXES, 0, 0, tiled=True)
    half, squares = sum_rows(recv.reshape(DEVICES * BLOCK, 128))
    part = lax.all_to_all(squares.reshape(DEVICES, 1, 128), AXES, 0, 0, tiled=True)
    other = lax.ppermute(half, "rep", [(0, 1), (1, 0)])
    return update(part.reshape(DEVICES, 128), half, other, table, moment, second)


def solution(mesh):
    return jax.shard_map(
        local,
        mesh=mesh,
        in_specs=(
            P(("dp", "rep"), None),
            P(("dp", "rep"), None),
            P(("dp", "rep")),
            P("dp", None),
            P("dp", None),
            P("dp", None),
        ),
        out_specs=(P("dp", None), P("dp", None), P("dp", None)),
        check_vma=False,
    )
```

time: 126 us -> 80.2 us (0.64)
  other arithmetic: 35.6 us -> 0 us
  waiting for transfers between devices: 29.9 us -> 0.01 us
  blocking collectives: 28 us -> 54.5 us
  Pallas kernels: 0 us -> 18.5 us
  starting transfers between devices: 17.7 us -> 1.46 us
  local copies, waits for them, and re-layouts: 12.5 us -> 4.77 us
    all_to_all x2 -> x0, waiting for transfers between devices: 29.9 us -> none  [the longest x1 25.9 us: local(): lax.all_to_all(send_rows.reshape(owners, capacity, feature_cols), 'dp', s...]
    all_to_all x2, blocking collectives: 28 us -> 54.5 us  [the longest x1 42.1 us: local(): lax.all_to_all(send.reshape(DEVICES, 1, BLOCK * 128), AXES, 0, 0, tiled=T...]
    pallas_call x0 -> x3, Pallas kernels: none -> 18.5 us  [the longest x1 6.8 us: update(): pl.pallas_call(update_kernel, out_shape=(shape,) * 3, in_specs=[pl.BlockS...]
    all_to_all x2 -> x0, starting transfers between devices: 17.7 us -> none  [the longest x1 12 us: local(): lax.all_to_all(send_ids.reshape(owners, capacity), 'dp', split_axis=0, co...]
    reduce_sum x4 -> x0, other arithmetic: 12.1 us -> none  [the longest x2 7.48 us: of_everyone(): return copy_for_each(value, axis).sum(axis=0)]
    sub x1 -> x0, other arithmetic: 11.2 us -> none  [adamw(): new_table = table_rows - 0.01 * (update + 0.01 * table_rows)]
    scatter-add x1 -> x0, other arithmetic: 8.95 us -> none  [accumulate(): jnp.zeros((row_count, feature_cols), jnp.float32).at[slot_index]]
    scatter x2 -> x0, local copies, waits for them, and re-layouts: 6.92 us -> none  [the longest x1 4.32 us: local(): jnp.zeros((owners * capacity, feature_cols), jnp.float32).at[destination]]
  transfers between devices with their start and end apart: 2 -> 1, of which waited for: 2 -> 0; matrix products, arithmetic and copies ran while one was open for 5% -> 0% of each run, Pallas kernels for 0% -> 0%
where the time goes in v1:
time: 80.2 us; the launch traced here: 79.9 us
  blocking collectives  54.5 us (68%)
  Pallas kernels  18.5 us (23%)
  local copies, waits for them, and re-layouts  4.77 us (6%)
  starting transfers between devices  1.46 us (2%)
    all_to_all x1, blocking collectives, local(): lax.all_to_all(send.reshape(DEVICES, 1, BLOCK * 128), AXES, 0, 0, tiled=T...  42.1 us
    all_to_all x1, blocking collectives, local(): lax.all_to_all(squares.reshape(DEVICES, 1, 128), AXES, 0, 0, tiled=True)  12.4 us
    pallas_call x1, Pallas kernels, update(): pl.pallas_call(update_kernel, out_shape=(shape,) * 3, in_specs=[pl.BlockS...  6.8 us
    pallas_call x1, Pallas kernels, pack(): pl.pallas_call(pack_kernel, out_shape=jax.ShapeDtypeStruct((DEVICES * BLO...  6.67 us
    pallas_call x1, Pallas kernels, sum_rows(): pl.pallas_call(sum_kernel, out_shape=(jax.ShapeDtypeStruct((ROWS, 256), j...  5.02 us
    unnamed x12, local copies, waits for them, and re-layouts  4.77 us
  transfers between devices with their start and end apart: 1, of which 0 were waited for; matrix products, arithmetic and copies ran while one was open for 0% of the time, Pallas kernels for 0%

profile of v1, /device:TPU:1, one launch (start us, length us, event | category | flops | bytes accessed | tf_op | source)
XLA Modules:
  0.0 79.9 jit_solution(4744120283898336288)
XLA Ops:
  0.6 0.0 copy-start.3
  0.6 1.2 %copy-done.3 = f32[512,512]{1,0:T(8,128)S(1)} copy-done((f32[512,512]{1,0:T(8,128)S(1)}, f32[512,512]{1,0:T(8,128)}, u32[]{:S(2)}) %copy-start.3) | copy-done | bytes 1048600
  1.9 0.0 copy-start.4
  1.9 0.7 copy-done.4
  2.5 0.0 copy-start.5
  2.5 0.7 copy-done.5
  3.2 0.0 copy-start
  3.2 0.0 copy-start.1
  3.2 6.7 %pack.1 = f32[4224,128]{1,0:T(8,128)S(1)} custom-call(s32[512]{0:T(512)S(1)} %bitcast.17, s32[512]{0:T(512)S(1)} %copy-done.5, f32[2048,128]{1,0:T(8,128)S(1)} %bitcast.14), custom_call_target="tpu_custom_call" | custom-call | tf_op jit(solution)/shard_map/pack/pallas_call | solution.py:60
  9.9 42.1 %all_to_all.10 = f32[128,1,4224]{2,1,0:T(1,128)S(1)} all-to-all(f32[128,1,4224]{2,1,0:T(1,128)S(1)} %bitcast.13), channel_id=1, replica_groups=mesh['dp'=64,'rep'=2] {'dp','rep'}, dimensions={0} | all-to-all | bytes 4325376 | tf_op jit(solution)/shard_map/all_to_all | solution.py:210
  52.0 5.0 %sum_rows.1 = (f32[2048,256]{1,0:T(8,128)S(1)}, f32[128,128]{1,0:T(8,128)S(1)}) custom-call(f32[4224,128]{1,0:T(8,128)S(1)} %bitcast.12), custom_call_target="tpu_custom_call" | custom-call | tf_op jit(solution)/shard_map/sum_rows/pallas_call | solution.py:129
  57.0 1.5 %collective-permute-start = (f32[2048,256]{1,0:T(8,128)S(1)}, f32[2048,256]{1,0:T(8,128)S(1)}, u32[]{:S(2)}, u32[]{:S(2)}) collective-permute-start(f32[2048,256]{1,0:T(8,128)S(1)} %get-tuple-element.6.own), channel_id=1, source_target_pairs={{0,1},{1,0},{2,3},{3,2},{4,5},{5,4},{6,7},{7,6},{8,9},{9,8},{10,11... | collective-permute-start | bytes 6291464 | tf_op jit(solution)/shard_map/ppermute | solution.py:213
  58.5 12.4 %all_to_all.11 = f32[128,1,128]{2,1,0:T(1,128)S(1)} all-to-all(f32[128,1,128]{2,1,0:T(1,128)S(1)} %bitcast.16), channel_id=1, replica_groups=mesh['dp'=64,'rep'=2] {'dp','rep'}, dimensions={0} | all-to-all | bytes 131072 | tf_op jit(solution)/shard_map/all_to_all | solution.py:212
  70.9 0.0 collective-permute-done.other
  70.9 0.0 copy-done
  70.9 0.0 copy-done.1
  70.9 0.0 copy-start.2
  70.9 2.2 %copy-done.2 = f32[2048,512]{1,0:T(8,128)S(1)} copy-done((f32[2048,512]{1,0:T(8,128)S(1)}, f32[2048,512]{1,0:T(8,128)}, u32[]{:S(2)}) %copy-start.2) | copy-done | bytes 4194328
  73.1 6.8 %update.1 = (f32[2048,512]{1,0:T(8,128)}, f32[2048,512]{1,0:T(8,128)}, f32[2048,512]{1,0:T(8,128)}) custom-call(f32[128,128]{1,0:T(8,128)S(1)} %bitcast.15, f32[2048,256]{1,0:T(8,128)S(1)} %get-tuple-element.6.own, f32[2048,256]{1,0:T(8,128)S(1)} %collective-permute-done.other, f32[2048,512]{1,0:T(8,128)S(1)} %copy-done, f32[2048,512]{1,0:T(8,128)S(1)} %copy-done.1, ...), custom_call_target="tpu_custom_call" | custom-call | tf_op jit(solution)/shard_map/update/pallas_call | solution.py:195
Async XLA Ops:
  0.6 1.2 %copy-start.3 = (f32[512,512]{1,0:T(8,128)S(1)}, f32[512,512]{1,0:T(8,128)}, u32[]{:S(2)}) copy-start(f32[512,512]{1,0:T(8,128)} %param.6) | copy-start | bytes 3145732
  1.9 0.7 copy-start.4
  2.5 0.7 copy-start.5
  3.2 67.6 %copy-start = (f32[2048,512]{1,0:T(8,128)S(1)}, f32[2048,512]{1,0:T(8,128)}, u32[]{:S(2)}) copy-start(f32[2048,512]{1,0:T(8,128)} %table.1) | copy-start | bytes 12582916
  3.2 67.6 %copy-start.1 = (f32[2048,512]{1,0:T(8,128)S(1)}, f32[2048,512]{1,0:T(8,128)}, u32[]{:S(2)}) copy-start(f32[2048,512]{1,0:T(8,128)} %moment.1) | copy-start | bytes 12582916
  57.0 13.8 %collective-permute-start = (f32[2048,256]{1,0:T(8,128)S(1)}, f32[2048,256]{1,0:T(8,128)S(1)}, u32[]{:S(2)}, u32[]{:S(2)}) collective-permute-start(f32[2048,256]{1,0:T(8,128)S(1)} %get-tuple-element.6.own), channel_id=1, source_target_pairs={{0,1},{1,0},{2,3},{3,2},{4,5},{5,4},{6,7},{7,6},{8,9},{9,8},{10,11... | collective-permute-start | bytes 6291464 | tf_op jit(solution)/shard_map/ppermute | solution.py:213
  70.9 2.2 %copy-start.2 = (f32[2048,512]{1,0:T(8,128)S(1)}, f32[2048,512]{1,0:T(8,128)}, u32[]{:S(2)}) copy-start(f32[2048,512]{1,0:T(8,128)} %second.1) | copy-start | bytes 12582916

commit v2 on v1

v2 whole, which is shorter than its diff:
```python
import jax
import jax.numpy as jnp
from jax import lax
from jax.experimental import pallas as pl
from jax.experimental.pallas import tpu as pltpu
from jax.sharding import PartitionSpec as P

VOCAB = 131072
ADAM_STEP = 100
LW = 512
OWNERS = 64
SLOTS = 16
TOKENS = 512
ROWS = 2048
DEVICES = 128
BLOCK = 2 * SLOTS + 1
PITCH = 2064
CHAINS = 8
CHUNK = 16
AXES = ("dp", "rep")
VMEM = pltpu.MemorySpace.VMEM
SMEM = pltpu.MemorySpace.SMEM
HBM = pltpu.MemorySpace.HBM


def pack_kernel(owner, row, x, send, owner_v, row_v, x_v, dest_v, dest_s, sems):
    loads = [
        pltpu.make_async_copy(a, b, sems.at[n])
        for n, (a, b) in enumerate(((owner, owner_v), (row, row_v), (x, x_v)))
    ]
    for load in loads:
        load.start()
    early = lax.broadcasted_iota(jnp.int32, (128, 128), 0)
    late = lax.broadcasted_iota(jnp.int32, (128, 128), 1)
    before = jnp.where(early < late, 1.0, 0.0).astype(jnp.bfloat16)
    ones = jnp.ones((128, 128), jnp.bfloat16)
    who = lax.broadcasted_iota(jnp.int32, (OWNERS, 128), 0)
    base = (who * (2 * BLOCK)).astype(jnp.float32)
    mine = lax.rem(lax.axis_index("dp") * 2 + lax.axis_index("rep"), 8)
    loads[0].wait()
    masks = [who == owner_v[i : i + 1, :] for i in range(4)]
    hots = [jnp.where(mask, 1.0, 0.0).astype(jnp.bfloat16) for mask in masks]
    hot = jnp.concatenate(hots, axis=0)
    inside = jnp.dot(hot, before, preferred_element_type=jnp.float32)
    counts = jnp.dot(hot, ones, preferred_element_type=jnp.float32)
    seen = jnp.zeros((OWNERS, 128), jnp.float32)
    positions = []
    for i in range(4):
        part = slice(i * OWNERS, (i + 1) * OWNERS)
        at = jnp.where(masks[i], inside[part] + seen, 0.0)
        positions.append(jnp.sum(at, axis=0, keepdims=True))
        start = jnp.sum(jnp.where(masks[i], base, 0.0), axis=0, keepdims=True)
        dest_v[i : i + 1, :] = (start + positions[i]).astype(jnp.int32)
        seen = seen + counts[part]
    move = pltpu.make_async_copy(dest_v, dest_s, sems.at[3])
    move.start()
    loads[1].wait()
    lines = early - mine * SLOTS
    ids = jnp.zeros((OWNERS, 256), jnp.float32)
    for i in range(4):
        left = ROWS - row_v[i : i + 1, :]
        here = lines == positions[i].astype(jnp.int32)
        high = jnp.where(here, (left >> 4).astype(jnp.float32), 0.0)
        low = jnp.where(here, (left & 15).astype(jnp.float32), 0.0)
        both = jnp.concatenate([high, low], axis=0).astype(jnp.bfloat16)
        ids = ids + lax.dot_general(
            hots[i], both, (((1,), (1,)), ((), ())), preferred_element_type=jnp.float32
        )
    ids = ROWS - (16.0 * ids[:, :128] + ids[:, 128:])
    lane = lax.broadcasted_iota(jnp.int32, (OWNERS, 128), 1)
    ids = jnp.where((lane >> 4) == mine, ids, 0.0)
    for a in range(OWNERS // 8):
        for h in range(2):
            spot = (16 * a + h) * BLOCK + 2 * SLOTS
            send[pl.ds(spot, 8, stride=2 * BLOCK), :] = ids[8 * a : 8 * a + 8]
    loads[2].wait()
    move.wait()

    def tokens(step, _):
        rows = x_v.at[pl.ds(pl.multiple_of(step * 512, 512), 512)]
        for k in range(128):
            block = dest_s[step, k]
            base = k // 8 * 32 + k % 8
            send[pl.ds(block, 2, stride=SLOTS), :] = rows[pl.ds(base, 2, stride=8), :]
            send[pl.ds(block + BLOCK, 2, stride=SLOTS), :] = rows[pl.ds(base + 16, 2, stride=8), :]
        return 0

    lax.fori_loop(0, TOKENS // 128, tokens, 0)


def pack(owner, row, x):
    return pl.pallas_call(
        pack_kernel,
        out_shape=jax.ShapeDtypeStruct((DEVICES * BLOCK, 128), jnp.float32),
        in_specs=[pl.BlockSpec(memory_space=HBM)] * 3,
        out_specs=pl.BlockSpec(memory_space=VMEM),
        scratch_shapes=[
            pltpu.VMEM((4, 128), jnp.int32),
            pltpu.VMEM((4, 128), jnp.int32),
            pltpu.VMEM((4 * TOKENS, 128), jnp.float32),
            pltpu.VMEM((4, 128), jnp.int32),
            pltpu.SMEM((4, 128), jnp.int32),
            pltpu.SemaphoreType.DMA((4,)),
        ],
        compiler_params=pltpu.CompilerParams(vmem_limit_bytes=5 * 2**20),
        name="pack",
    )(*(pltpu.with_memory_space_constraint(a, HBM) for a in (owner, row, x)))


def sum_kernel(recv, second, half, squares, second_v, ids_v, ids_s, sem, second_sem, *sums):
    fetch = pltpu.make_async_copy(second, second_v, second_sem)
    fetch.start()
    for g in range(16):
        lines = recv[pl.ds(g * 8 * BLOCK + 2 * SLOTS, 8, stride=BLOCK), :]
        ids_v[g : g + 1, :] = jnp.sum(lines, axis=0, keepdims=True).astype(jnp.int32)
    copy = pltpu.make_async_copy(ids_v, ids_s, sem)
    copy.start()

    def clear(i, _):
        for total in sums:
            for k in range(8):
                total[pl.ds(i * 64 + k * 8, 8), :] = jnp.zeros((8, 128), jnp.float32)
        return 0

    lax.fori_loop(0, 2 * PITCH // 64, clear, 0)
    for total in sums:
        for k in range(2 * PITCH // 64 * 64, 2 * PITCH, 8):
            total[k : k + 8, :] = jnp.zeros((8, 128), jnp.float32)
    copy.wait()
    groups = 16 // CHAINS

    def add(g, _):
        lines = [
            recv.at[pl.ds(pl.multiple_of((c * groups + g) * 8 * BLOCK, 8), 8 * BLOCK)]
            for c in range(CHAINS)
        ]
        for at in range(8 * SLOTS):
            line = at // SLOTS * BLOCK + at % SLOTS
            for c, total in enumerate(sums):
                spot = pl.ds(ids_s[c * groups + g, at], 2, stride=PITCH)
                total[spot, :] = total[spot, :] + lines[c][pl.ds(line, 2, stride=SLOTS), :]
        return 0

    lax.fori_loop(0, groups, add, 0)

    def fold(i, squared):
        squared = list(squared)
        for k in range(8):
            for j in range(2):
                at = pl.multiple_of(j * PITCH + i * 64 + k * 8, 8)
                parts = [total[pl.ds(at, 8), :] for total in sums]
                while len(parts) > 1:
                    parts = [a + b for a, b in zip(parts[::2], parts[1::2])]
                half[i * 8 + k, j] = parts[0]
                squared[k % 4] = squared[k % 4] + parts[0] * parts[0]
        return tuple(squared)

    zero = jnp.zeros((8, 128), jnp.float32)
    a, b, c, d = lax.fori_loop(0, ROWS // 64, fold, (zero,) * 4)
    squares[...] = jnp.broadcast_to(jnp.sum((a + b) + (c + d), axis=0, keepdims=True), squares.shape)
    fetch.wait()


def sum_rows(recv, second):
    return pl.pallas_call(
        sum_kernel,
        out_shape=(
            jax.ShapeDtypeStruct((ROWS // 8, 2, 8, 128), jnp.float32),
            jax.ShapeDtypeStruct((DEVICES, 128), jnp.float32),
            jax.ShapeDtypeStruct((ROWS // 8, 4, 8, 128), jnp.float32),
        ),
        in_specs=[pl.BlockSpec(memory_space=VMEM), pl.BlockSpec(memory_space=HBM)],
        out_specs=(pl.BlockSpec(memory_space=VMEM),) * 3,
        scratch_shapes=[
            pltpu.VMEM((16, 128), jnp.int32),
            pltpu.SMEM((16, 128), jnp.int32),
            pltpu.SemaphoreType.DMA,
            pltpu.SemaphoreType.DMA,
        ]
        + [pltpu.VMEM((2 * PITCH, 128), jnp.float32)] * CHAINS,
        compiler_params=pltpu.CompilerParams(vmem_limit_bytes=22 * 2**20),
        name="sum_rows",
    )(recv, pltpu.with_memory_space_constraint(second, HBM))


def update_kernel(part, own, other, table, moment, second, *rest):
    outs, bufs, sems = rest[0:3], rest[3:6], rest[6]
    total = jnp.sum(part[...], keepdims=True)
    limit = 0.5 * float(VOCAB * LW) ** 0.5
    clip = jnp.minimum(1.0, limit / (jnp.sqrt(total) + 1e-06))
    first_fix = 1.0 - 0.9**ADAM_STEP
    second_fix = 1.0 - 0.999**ADAM_STEP
    to_moment = jnp.broadcast_to(0.1 * clip, (8, 128))
    to_second = jnp.broadcast_to(0.001 * clip * clip, (8, 128))
    rep = lax.axis_index("rep")

    def tile(i, _):
        rows = pl.ds(i * 4, 4)
        for h, source in enumerate((own, other)):
            cols = pl.ds(jnp.where(rep == 0, h, 1 - h) * 2, 2)
            ins = [ref.at[rows, cols] for ref in (table, moment, second)]
            to = [ref.at[rows, cols] for ref in bufs]
            grads = source.at[rows]
            for k in range(4):
                for j in range(2):
                    g = grads[k, j]
                    nm = 0.9 * ins[1][k, j] + to_moment * g
                    nv = 0.999 * ins[2][k, j] + to_second * (g * g)
                    root = (nv * lax.rsqrt(nv)) * (1.0 / second_fix) ** 0.5 + 1e-08
                    to[1][k, j] = nm
                    to[2][k, j] = nv
                    step = (nm * (0.01 / first_fix)) / root
                    to[0][k, j] = (1.0 - 0.0001) * ins[0][k, j] - step
        return 0

    def copies(c):
        rows = pl.ds(c * CHUNK, CHUNK)
        return [
            pltpu.make_async_copy(buf.at[rows], out.at[rows], sems.at[n, c])
            for n, (buf, out) in enumerate(zip(bufs, outs))
        ]

    steps = CHUNK // 4
    for c in range(ROWS // 8 // CHUNK):
        lax.fori_loop(c * steps, (c + 1) * steps, tile, 0)
        for copy in copies(c):
            copy.start()
    for c in range(ROWS // 8 // CHUNK):
        for copy in copies(c):
            copy.wait()


def update(part, own, other, table, moment, second):
    shape = jax.ShapeDtypeStruct((ROWS // 8, 4, 8, 128), jnp.float32)
    return pl.pallas_call(
        update_kernel,
        out_shape=(shape,) * 3,
        in_specs=[pl.BlockSpec(memory_space=VMEM)] * 6,
        out_specs=(pl.BlockSpec(memory_space=pl.ANY),) * 3,
        scratch_shapes=[pltpu.VMEM((ROWS // 8, 4, 8, 128), jnp.float32)] * 3
        + [pltpu.SemaphoreType.DMA((3, ROWS // 8 // CHUNK))],
        compiler_params=pltpu.CompilerParams(vmem_limit_bytes=30 * 2**20),
        name="update",
    )(part, own, other, table, moment, second)


def tiles(array):
    rows, cols = array.shape
    return array.reshape(rows // 8, 8, cols // 128, 128).transpose(0, 2, 1, 3)


def local(row_grads, token_owner, token_row, table, moment, second):
    x = tiles(row_grads).reshape(4 * TOKENS, 128)
    send = pack(token_owner.reshape(4, 128), token_row.reshape(4, 128), x)
    recv = lax.all_to_all(send.reshape(DEVICES, 1, BLOCK * 128), AXES, 0, 0, tiled=True)
    half, squares, second = sum_rows(recv.reshape(DEVICES * BLOCK, 128), tiles(second))
    part = lax.all_to_all(squares.reshape(DEVICES, 1, 128), AXES, 0, 0, tiled=True)
    other = lax.ppermute(half, "rep", [(0, 1), (1, 0)])
    outs = update(part.reshape(DEVICES, 128), half, other, tiles(table), tiles(moment), second)
    return tuple(out.transpose(0, 2, 1, 3).reshape(ROWS, LW) for out in outs)


def solution(mesh):
    return jax.shard_map(
        local,
        mesh=mesh,
        in_specs=(
            P(("dp", "rep"), None),
            P(("dp", "rep"), None),
            P(("dp", "rep")),
            P("dp", None),
            P("dp", None),
            P("dp", None),
        ),
        out_specs=(P("dp", None), P("dp", None), P("dp", None)),
        check_vma=False,
    )
```

time: 80.2 us -> 68.6 us (0.86)
  Pallas kernels: 18.5 us -> 11.8 us
  local copies, waits for them, and re-layouts: 4.77 us -> 0.01 us
    unnamed x12 -> x4, local copies, waits for them, and re-layouts: 4.77 us -> 0.01 us
    pallas_call x1, Pallas kernels: 6.67 us -> 2.1 us  [pack(): pl.pallas_call(pack_kernel, out_shape=jax.ShapeDtypeStruct((DEVICES * BLO...]
    pallas_call x1, Pallas kernels: 6.8 us -> 5.27 us  [update(): pl.pallas_call(update_kernel, out_shape=(shape,) * 3, in_specs=[pl.BlockS...]
where the time goes in v2:
time: 68.6 us; the launch traced here: 68.4 us
  blocking collectives  54.5 us (79%)
  Pallas kernels  11.8 us (17%)
  starting transfers between devices  1.46 us (2%)
    all_to_all x1, blocking collectives, local(): lax.all_to_all(send.reshape(DEVICES, 1, BLOCK * 128), AXES, 0, 0, tiled=T...  42.1 us
    all_to_all x1, blocking collectives, local(): lax.all_to_all(squares.reshape(DEVICES, 1, 128), AXES, 0, 0, tiled=True)  12.4 us
    pallas_call x1, Pallas kernels, update(): pl.pallas_call(update_kernel, out_shape=(shape,) * 3, in_specs=[pl.BlockS...  5.27 us
    pallas_call x1, Pallas kernels, sum_rows(): pl.pallas_call(sum_kernel, out_shape=(jax.ShapeDtypeStruct((ROWS // 8, 2,...  4.43 us
    pallas_call x1, Pallas kernels, pack(): pl.pallas_call(pack_kernel, out_shape=jax.ShapeDtypeStruct((DEVICES * BLO...  2.1 us
    ppermute x1, starting transfers between devices, local(): other = lax.ppermute(half, 'rep', [(0, 1), (1, 0)])  1.46 us
  transfers between devices with their start and end apart: 1, of which 0 were waited for; matrix products, arithmetic and copies ran while one was open for 0% of the time, Pallas kernels for 0%

profile of v2, /device:TPU:1, one launch (start us, length us, event | category | flops | bytes accessed | tf_op | source)
XLA Modules:
  0.0 68.4 jit_solution(9766344416849251260)
XLA Ops:
  0.6 2.1 %pack.1 = f32[4224,128]{1,0:T(8,128)S(1)} custom-call(s32[4,128]{1,0:T(4,128)} %bitcast.39, s32[4,128]{1,0:T(4,128)} %bitcast.40, f32[2048,128]{1,0:T(8,128)} %bitcast.38), custom_call_target="tpu_custom_call" | custom-call | tf_op jit(solution)/shard_map/pack/pallas_call | solution.py:92
  2.7 0.0 copy-start.1
  2.8 42.1 %all_to_all.10 = f32[128,1,4224]{2,1,0:T(1,128)S(1)} all-to-all(f32[128,1,4224]{2,1,0:T(1,128)S(1)} %bitcast.32), channel_id=1, replica_groups=mesh['dp'=64,'rep'=2] {'dp','rep'}, dimensions={0} | all-to-all | bytes 4325376 | tf_op jit(solution)/shard_map/all_to_all | solution.py:255
  44.8 0.0 copy-start
  44.8 4.4 %sum_rows.1 = (f32[256,2,8,128]{3,2,1,0:T(8,128)S(1)}, f32[128,128]{1,0:T(8,128)S(1)}, f32[256,4,8,128]{3,2,1,0:T(8,128)S(1)}) custom-call(f32[4224,128]{1,0:T(8,128)S(1)} %bitcast.31, f32[256,4,8,128]{3,2,1,0:T(8,128)} %bitcast.37), custom_call_target="tpu_custom_call" | custom-call | tf_op jit(solution)/shard_map/sum_rows/pallas_call | solution.py:165
  49.3 1.5 %collective-permute-start = (f32[256,2,8,128]{3,2,1,0:T(8,128)S(1)}, f32[256,2,8,128]{3,2,1,0:T(8,128)S(1)}, u32[]{:S(2)}, u32[]{:S(2)}) collective-permute-start(f32[256,2,8,128]{3,2,1,0:T(8,128)S(1)} %get-tuple-element.10.own), channel_id=1, source_target_pairs={{0,1},{1,0},{2,3},{3,2},{4,5},{5,4},{6,7},{7,6},{8,9},{9,8},{10,11... | collective-permute-start | bytes 6291464 | tf_op jit(solution)/shard_map/ppermute | solution.py:258
  50.7 12.4 %all_to_all.11 = f32[128,1,128]{2,1,0:T(1,128)S(1)} all-to-all(f32[128,1,128]{2,1,0:T(1,128)S(1)} %bitcast.36), channel_id=1, replica_groups=mesh['dp'=64,'rep'=2] {'dp','rep'}, dimensions={0} | all-to-all | bytes 131072 | tf_op jit(solution)/shard_map/all_to_all | solution.py:257
  63.1 0.0 collective-permute-done.other
  63.1 0.0 copy-done.1
  63.1 0.0 copy-done
  63.1 5.3 %update.1 = (f32[256,4,8,128]{3,2,1,0:T(8,128)}, f32[256,4,8,128]{3,2,1,0:T(8,128)}, f32[256,4,8,128]{3,2,1,0:T(8,128)}) custom-call(f32[128,128]{1,0:T(8,128)S(1)} %bitcast.35, f32[256,2,8,128]{3,2,1,0:T(8,128)S(1)} %get-tuple-element.10.own, f32[256,2,8,128]{3,2,1,0:T(8,128)S(1)} %collective-permute-done.other, f32[256,4,8,128]{3,2,1,0:T(8,128)S(1)} %bitcast.33, ...), custom_call_target="tpu_custom_call" | custom-call | tf_op jit(solution)/shard_map/update/pallas_call | solution.py:235
Async XLA Ops:
  2.7 60.4 %copy-start.1 = (f32[2048,512]{1,0:T(8,128)S(1)}, f32[2048,512]{1,0:T(8,128)}, u32[]{:S(2)}) copy-start(f32[2048,512]{1,0:T(8,128)} %param.10) | copy-start | bytes 12582916
  44.8 18.3 %copy-start = (f32[2048,512]{1,0:T(8,128)S(1)}, f32[2048,512]{1,0:T(8,128)}, u32[]{:S(2)}) copy-start(f32[2048,512]{1,0:T(8,128)} %param.9) | copy-start | bytes 12582916
  49.3 13.8 %collective-permute-start = (f32[256,2,8,128]{3,2,1,0:T(8,128)S(1)}, f32[256,2,8,128]{3,2,1,0:T(8,128)S(1)}, u32[]{:S(2)}, u32[]{:S(2)}) collective-permute-start(f32[256,2,8,128]{3,2,1,0:T(8,128)S(1)} %get-tuple-element.10.own), channel_id=1, source_target_pairs={{0,1},{1,0},{2,3},{3,2},{4,5},{5,4},{6,7},{7,6},{8,9},{9,8},{10,11... | collective-permute-start | bytes 6291464 | tf_op jit(solution)/shard_map/ppermute | solution.py:258

commit v3 on v2

--- a/solution.py
+++ b/solution.py
@@ -15,15 +15,17 @@
 DEVICES = 128
 BLOCK = 2 * SLOTS + 1
 PITCH = 2064
-CHAINS = 8
-CHUNK = 16
+CHAINS = 6
+CHUNKS = (16, 24, 32, 48, 64, 72)
 AXES = ("dp", "rep")
 VMEM = pltpu.MemorySpace.VMEM
 SMEM = pltpu.MemorySpace.SMEM
 HBM = pltpu.MemorySpace.HBM
 
 
-def pack_kernel(owner, row, x, send, owner_v, row_v, x_v, dest_v, dest_s, sems):
+def pack_kernel(owner, row, x, send, *refs):
+    sums = refs[:CHAINS]
+    owner_v, row_v, x_v, dest_v, dest_s, sems = refs[CHAINS:]
     loads = [
         pltpu.make_async_copy(a, b, sems.at[n])
         for n, (a, b) in enumerate(((owner, owner_v), (row, row_v), (x, x_v)))
@@ -37,6 +39,14 @@
     who = lax.broadcasted_iota(jnp.int32, (OWNERS, 128), 0)
     base = (who * (2 * BLOCK)).astype(jnp.float32)
     mine = lax.rem(lax.axis_index("dp") * 2 + lax.axis_index("rep"), 8)
+
+    def clear(i, _):
+        for total in sums:
+            for k in range(4):
+                total[pl.ds(i * 32 + k * 8, 8), :] = jnp.zeros((8, 128), jnp.float32)
+        return 0
+
+    lax.fori_loop(0, 2 * PITCH // 64, clear, 0)
     loads[0].wait()
     masks = [who == owner_v[i : i + 1, :] for i in range(4)]
     hots = [jnp.where(mask, 1.0, 0.0).astype(jnp.bfloat16) for mask in masks]
@@ -68,11 +78,13 @@
         )
     ids = ROWS - (16.0 * ids[:, :128] + ids[:, 128:])
     lane = lax.broadcasted_iota(jnp.int32, (OWNERS, 128), 1)
+    ids = jnp.where(ids == ROWS, (ROWS + (lane & 15)).astype(jnp.float32), ids)
     ids = jnp.where((lane >> 4) == mine, ids, 0.0)
     for a in range(OWNERS // 8):
         for h in range(2):
             spot = (16 * a + h) * BLOCK + 2 * SLOTS
             send[pl.ds(spot, 8, stride=2 * BLOCK), :] = ids[8 * a : 8 * a + 8]
+    lax.fori_loop(2 * PITCH // 64, 2 * PITCH // 32, clear, 0)
     loads[2].wait()
     move.wait()
 
@@ -91,9 +103,10 @@
 def pack(owner, row, x):
     return pl.pallas_call(
         pack_kernel,
-        out_shape=jax.ShapeDtypeStruct((DEVICES * BLOCK, 128), jnp.float32),
+        out_shape=(jax.ShapeDtypeStruct((DEVICES * BLOCK, 128), jnp.float32),)
+        + (jax.ShapeDtypeStruct((2 * PITCH, 128), jnp.float32),) * CHAINS,
         in_specs=[pl.BlockSpec(memory_space=HBM)] * 3,
-        out_specs=pl.BlockSpec(memory_space=VMEM),
+        out_specs=(pl.BlockSpec(memory_space=VMEM),) * (1 + CHAINS),
         scratch_shapes=[
             pltpu.VMEM((4, 128), jnp.int32),
             pltpu.VMEM((4, 128), jnp.int32),
@@ -102,46 +115,45 @@
             pltpu.SMEM((4, 128), jnp.int32),
             pltpu.SemaphoreType.DMA((4,)),
         ],
-        compiler_params=pltpu.CompilerParams(vmem_limit_bytes=5 * 2**20),
+        compiler_params=pltpu.CompilerParams(vmem_limit_bytes=20 * 2**20),
         name="pack",
     )(*(pltpu.with_memory_space_constraint(a, HBM) for a in (owner, row, x)))
 
 
-def sum_kernel(recv, second, half, squares, second_v, ids_v, ids_s, sem, second_sem, *sums):
-    fetch = pltpu.make_async_copy(second, second_v, second_sem)
-    fetch.start()
+def sum_kernel(recv, second, *refs):
+    half, squares, second_v = refs[CHAINS : CHAINS + 3]
+    sums = refs[CHAINS + 3 : 2 * CHAINS + 3]
+    ids_v, ids_s, id_sems, sem = refs[2 * CHAINS + 3 :]
+    fetch = pltpu.make_async_copy(second, second_v, sem)
+    def move(q):
+        part = pl.ds(pl.multiple_of(q * 8, 8), 8)
+        return pltpu.make_async_copy(ids_v.at[part], ids_s.at[part], id_sems.at[q])
+
     for g in range(16):
         lines = recv[pl.ds(g * 8 * BLOCK + 2 * SLOTS, 8, stride=BLOCK), :]
-        ids_v[g : g + 1, :] = jnp.sum(lines, axis=0, keepdims=True).astype(jnp.int32)
-    copy = pltpu.make_async_copy(ids_v, ids_s, sem)
-    copy.start()
-
-    def clear(i, _):
-        for total in sums:
-            for k in range(8):
-                total[pl.ds(i * 64 + k * 8, 8), :] = jnp.zeros((8, 128), jnp.float32)
-        return 0
-
-    lax.fori_loop(0, 2 * PITCH // 64, clear, 0)
-    for total in sums:
-        for k in range(2 * PITCH // 64 * 64, 2 * PITCH, 8):
-            total[k : k + 8, :] = jnp.zeros((8, 128), jnp.float32)
-    copy.wait()
-    groups = 16 // CHAINS
+        at = g // 4 * 8 + g % 4
+        ids_v[at : at + 1, :] = jnp.sum(lines, axis=0, keepdims=True).astype(jnp.int32)
+        if g % 4 == 3:
+            move(g // 4).start()
+
+    fetch.start()
 
     def add(g, _):
-        lines = [
-            recv.at[pl.ds(pl.multiple_of((c * groups + g) * 8 * BLOCK, 8), 8 * BLOCK)]
-            for c in range(CHAINS)
-        ]
+        q, k = g >> 2, g & 3
+
+        @pl.when(k == 0)
+        def _():
+            move(q).wait()
+
+        lines = recv.at[pl.ds(pl.multiple_of(g * 8 * BLOCK, 8), 8 * BLOCK)]
         for at in range(8 * SLOTS):
+            total = sums[at % CHAINS]
             line = at // SLOTS * BLOCK + at % SLOTS
-            for c, total in enumerate(sums):
-                spot = pl.ds(ids_s[c * groups + g, at], 2, stride=PITCH)
-                total[spot, :] = total[spot, :] + lines[c][pl.ds(line, 2, stride=SLOTS), :]
-        return 0
-
-    lax.fori_loop(0, groups, add, 0)
+            spot = pl.ds(ids_s[q * 8 + k, at], 2, stride=PITCH)
+            total[spot, :] = total[spot, :] + lines[pl.ds(line, 2, stride=SLOTS), :]
+        return 0
+
+    lax.fori_loop(0, 16, add, 0)
 
     def fold(i, squared):
         squared = list(squared)
@@ -150,7 +162,7 @@
                 at = pl.multiple_of(j * PITCH + i * 64 + k * 8, 8)
                 parts = [total[pl.ds(at, 8), :] for total in sums]
                 while len(parts) > 1:
-                    parts = [a + b for a, b in zip(parts[::2], parts[1::2])]
+                    parts = [sum(parts[k : k + 2]) for k in range(0, len(parts), 2)]
                 half[i * 8 + k, j] = parts[0]
                 squared[k % 4] = squared[k % 4] + parts[0] * parts[0]
         return tuple(squared)
@@ -161,26 +173,29 @@
     fetch.wait()
 
 
-def sum_rows(recv, second):
+def sum_rows(recv, second, sums):
+    total = jax.ShapeDtypeStruct((2 * PITCH, 128), jnp.float32)
     return pl.pallas_call(
         sum_kernel,
         out_shape=(
             jax.ShapeDtypeStruct((ROWS // 8, 2, 8, 128), jnp.float32),
             jax.ShapeDtypeStruct((DEVICES, 128), jnp.float32),
             jax.ShapeDtypeStruct((ROWS // 8, 4, 8, 128), jnp.float32),
-        ),
-        in_specs=[pl.BlockSpec(memory_space=VMEM), pl.BlockSpec(memory_space=HBM)],
-        out_specs=(pl.BlockSpec(memory_space=VMEM),) * 3,
+        )
+        + (total,) * CHAINS,
+        in_specs=[pl.BlockSpec(memory_space=VMEM), pl.BlockSpec(memory_space=HBM)]
+        + [pl.BlockSpec(memory_space=VMEM)] * CHAINS,
+        out_specs=(pl.BlockSpec(memory_space=VMEM),) * (3 + CHAINS),
         scratch_shapes=[
-            pltpu.VMEM((16, 128), jnp.int32),
-            pltpu.SMEM((16, 128), jnp.int32),
+            pltpu.VMEM((32, 128), jnp.int32),
+            pltpu.SMEM((32, 128), jnp.int32),
+            pltpu.SemaphoreType.DMA((4,)),
             pltpu.SemaphoreType.DMA,
-            pltpu.SemaphoreType.DMA,
-        ]
-        + [pltpu.VMEM((2 * PITCH, 128), jnp.float32)] * CHAINS,
+        ],
+        input_output_aliases={2 + c: 3 + c for c in range(CHAINS)},
         compiler_params=pltpu.CompilerParams(vmem_limit_bytes=22 * 2**20),
         name="sum_rows",
-    )(recv, pltpu.with_memory_space_constraint(second, HBM))
+    )(recv, pltpu.with_memory_space_constraint(second, HBM), *sums)
 
 
 def update_kernel(part, own, other, table, moment, second, *rest):
@@ -213,21 +228,24 @@
                     to[0][k, j] = (1.0 - 0.0001) * ins[0][k, j] - step
         return 0
 
-    def copies(c):
-        rows = pl.ds(c * CHUNK, CHUNK)
+    def copies(c, first):
+        rows = pl.ds(first, CHUNKS[c])
         return [
             pltpu.make_async_copy(buf.at[rows], out.at[rows], sems.at[n, c])
             for n, (buf, out) in enumerate(zip(bufs, outs))
         ]
 
-    steps = CHUNK // 4
-    for c in range(ROWS // 8 // CHUNK):
-        lax.fori_loop(c * steps, (c + 1) * steps, tile, 0)
-        for copy in copies(c):
+    first = 0
+    started = []
+    for c, count in enumerate(CHUNKS):
+        lax.fori_loop(first // 4, (first + count) // 4, tile, 0)
+        chunk = copies(c, first)
+        for copy in chunk:
             copy.start()
-    for c in range(ROWS // 8 // CHUNK):
-        for copy in copies(c):
-            copy.wait()
+        started += chunk
+        first += count
+    for copy in started:
+        copy.wait()
 
 
 def update(part, own, other, table, moment, second):
@@ -238,7 +256,7 @@
         in_specs=[pl.BlockSpec(memory_space=VMEM)] * 6,
         out_specs=(pl.BlockSpec(memory_space=pl.ANY),) * 3,
         scratch_shapes=[pltpu.VMEM((ROWS // 8, 4, 8, 128), jnp.float32)] * 3
-        + [pltpu.SemaphoreType.DMA((3, ROWS // 8 // CHUNK))],
+        + [pltpu.SemaphoreType.DMA((3, len(CHUNKS)))],
         compiler_params=pltpu.CompilerParams(vmem_limit_bytes=30 * 2**20),
         name="update",
     )(part, own, other, table, moment, second)
@@ -251,9 +269,10 @@
 
 def local(row_grads, token_owner, token_row, table, moment, second):
     x = tiles(row_grads).reshape(4 * TOKENS, 128)
-    send = pack(token_owner.reshape(4, 128), token_row.reshape(4, 128), x)
+    send, *sums = pack(token_owner.reshape(4, 128), token_row.reshape(4, 128), x)
     recv = lax.all_to_all(send.reshape(DEVICES, 1, BLOCK * 128), AXES, 0, 0, tiled=True)
-    half, squares, second = sum_rows(recv.reshape(DEVICES * BLOCK, 128), tiles(second))
+    lines = recv.reshape(DEVICES * BLOCK, 128)
+    half, squares, second = sum_rows(lines, tiles(second), sums)[:3]
     part = lax.all_to_all(squares.reshape(DEVICES, 1, 128), AXES, 0, 0, tiled=True)
     other = lax.ppermute(half, "rep", [(0, 1), (1, 0)])
     outs = update(part.reshape(DEVICES, 128), half, other, tiles(table), tiles(moment), second)

time: 68.6 us -> 67.7 us (0.987)
  Pallas kernels: 11.8 us -> 11 us
    pallas_call x1, Pallas kernels: 4.43 us -> 3.65 us  [sum_rows(): pl.pallas_call(sum_kernel, out_shape=(jax.ShapeDtypeStruct((ROWS // 8, 2,...]
where the time goes in v3:
time: 67.7 us; the launch traced here: 67.6 us
  blocking collectives  54.5 us (81%)
  Pallas kernels  11 us (16%)
  starting transfers between devices  1.46 us (2%)
    all_to_all x1, blocking collectives, local(): lax.all_to_all(send.reshape(DEVICES, 1, BLOCK * 128), AXES, 0, 0, tiled=T...  42.1 us
    all_to_all x1, blocking collectives, local(): lax.all_to_all(squares.reshape(DEVICES, 1, 128), AXES, 0, 0, tiled=True)  12.4 us
    pallas_call x1, Pallas kernels, update(): pl.pallas_call(update_kernel, out_shape=(shape,) * 3, in_specs=[pl.BlockS...  5.06 us
    pallas_call x1, Pallas kernels, sum_rows(): pl.pallas_call(sum_kernel, out_shape=(jax.ShapeDtypeStruct((ROWS // 8, 2,...  3.65 us
    pallas_call x1, Pallas kernels, pack(): pl.pallas_call(pack_kernel, out_shape=(jax.ShapeDtypeStruct((DEVICES * BL...  2.28 us
    ppermute x1, starting transfers between devices, local(): other = lax.ppermute(half, 'rep', [(0, 1), (1, 0)])  1.46 us
  transfers between devices with their start and end apart: 1, of which 0 were waited for; matrix products, arithmetic and copies ran while one was open for 0% of the time, Pallas kernels for 0%

profile of v3, /device:TPU:1, one launch (start us, length us, event | category | flops | bytes accessed | tf_op | source)
XLA Modules:
  0.0 67.6 jit_solution(17209048709599170661)
XLA Ops:
  0.6 2.3 %pack.1 = (f32[4224,128]{1,0:T(8,128)S(1)}, f32[4128,128]{1,0:T(8,128)S(1)}, f32[4128,128]{1,0:T(8,128)S(1)}, f32[4128,128]{1,0:T(8,128)S(1)}, f32[4128,128]{1,0...) custom-call(s32[4,128]{1,0:T(4,128)} %bitcast.39, s32[4,128]{1,0:T(4,128)} %bitcast.40, f32[2048,128]{1,0:T(8,128)} %bitcast.38), custom_call_target="tpu_custom_call" | custom-call | tf_op jit(solution)/shard_map/pack/pallas_call | solution.py:104
  2.9 42.1 %all_to_all.10 = f32[128,1,4224]{2,1,0:T(1,128)S(1)} all-to-all(f32[128,1,4224]{2,1,0:T(1,128)S(1)} %bitcast.34), channel_id=1, replica_groups=mesh['dp'=64,'rep'=2] {'dp','rep'}, dimensions={0} | all-to-all | bytes 4325376 | tf_op jit(solution)/shard_map/all_to_all | solution.py:273
  45.0 0.0 copy-start
  45.0 0.0 copy-start.1
  45.0 3.7 %sum_rows.1 = (f32[256,2,8,128]{3,2,1,0:T(8,128)S(1)}, f32[128,128]{1,0:T(8,128)S(1)}, f32[256,4,8,128]{3,2,1,0:T(8,128)S(1)}, f32[4128,128]{1,0:T(8,128)S(1)}, ...) custom-call(f32[4224,128]{1,0:T(8,128)S(1)} %bitcast.31, ...), custom_call_target="tpu_custom_call", output_to_operand_aliasing={{3}: (2, {}), {4}: (3, {}), {5}: (4, {}), {6}: (5, {}), {7}... | custom-call | tf_op jit(solution)/shard_map/sum_rows/pallas_call | solution.py:178
  48.7 1.5 %collective-permute-start = (f32[256,2,8,128]{3,2,1,0:T(8,128)S(1)}, f32[256,2,8,128]{3,2,1,0:T(8,128)S(1)}, u32[]{:S(2)}, u32[]{:S(2)}) collective-permute-start(f32[256,2,8,128]{3,2,1,0:T(8,128)S(1)} %get-tuple-element.24.own), channel_id=1, source_target_pairs={{0,1},{1,0},{2,3},{3,2},{4,5},{5,4},{6,7},{7,6},{8,9},{9,8},{10,11... | collective-permute-start | bytes 6291464 | tf_op jit(solution)/shard_map/ppermute | solution.py:277
  50.1 12.4 %all_to_all.11 = f32[128,1,128]{2,1,0:T(1,128)S(1)} all-to-all(f32[128,1,128]{2,1,0:T(1,128)S(1)} %bitcast.36), channel_id=1, replica_groups=mesh['dp'=64,'rep'=2] {'dp','rep'}, dimensions={0} | all-to-all | bytes 131072 | tf_op jit(solution)/shard_map/all_to_all | solution.py:276
  62.5 0.0 collective-permute-done.other
  62.5 0.0 copy-done
  62.5 0.0 copy-done.1
  62.5 5.1 %update.1 = (f32[256,4,8,128]{3,2,1,0:T(8,128)}, f32[256,4,8,128]{3,2,1,0:T(8,128)}, f32[256,4,8,128]{3,2,1,0:T(8,128)}) custom-call(f32[128,128]{1,0:T(8,128)S(1)} %bitcast.35, f32[256,2,8,128]{3,2,1,0:T(8,128)S(1)} %get-tuple-element.24.own, f32[256,2,8,128]{3,2,1,0:T(8,128)S(1)} %collective-permute-done.other, f32[256,4,8,128]{3,2,1,0:T(8,128)S(1)} %bitcast.32, ...), custom_call_target="tpu_custom_call" | custom-call | tf_op jit(solution)/shard_map/update/pallas_call | solution.py:253
Async XLA Ops:
  45.0 17.5 %copy-start = (f32[2048,512]{1,0:T(8,128)S(1)}, f32[2048,512]{1,0:T(8,128)}, u32[]{:S(2)}) copy-start(f32[2048,512]{1,0:T(8,128)} %param.9) | copy-start | bytes 12582916
  45.0 17.5 %copy-start.1 = (f32[2048,512]{1,0:T(8,128)S(1)}, f32[2048,512]{1,0:T(8,128)}, u32[]{:S(2)}) copy-start(f32[2048,512]{1,0:T(8,128)} %param.10) | copy-start | bytes 12582916
  48.7 13.8 %collective-permute-start = (f32[256,2,8,128]{3,2,1,0:T(8,128)S(1)}, f32[256,2,8,128]{3,2,1,0:T(8,128)S(1)}, u32[]{:S(2)}, u32[]{:S(2)}) collective-permute-start(f32[256,2,8,128]{3,2,1,0:T(8,128)S(1)} %get-tuple-element.24.own), channel_id=1, source_target_pairs={{0,1},{1,0},{2,3},{3,2},{4,5},{5,4},{6,7},{7,6},{8,9},{9,8},{10,11... | collective-permute-start | bytes 6291464 | tf_op jit(solution)/shard_map/ppermute | solution.py:277

commit v4 on v3

--- a/solution.py
+++ b/solution.py
@@ -16,7 +16,7 @@
 BLOCK = 2 * SLOTS + 1
 PITCH = 2064
 CHAINS = 6
-CHUNKS = (16, 24, 32, 48, 64, 72)
+CHUNKS = (8, 16, 24, 36, 52, 64, 56)
 AXES = ("dp", "rep")
 VMEM = pltpu.MemorySpace.VMEM
 SMEM = pltpu.MemorySpace.SMEM
@@ -132,43 +132,37 @@
     for g in range(16):
         lines = recv[pl.ds(g * 8 * BLOCK + 2 * SLOTS, 8, stride=BLOCK), :]
         at = g // 4 * 8 + g % 4
-        ids_v[at : at + 1, :] = jnp.sum(lines, axis=0, keepdims=True).astype(jnp.int32)
+        ids_v[at : at + 1, :] = (2 * jnp.sum(lines, axis=0, keepdims=True)).astype(jnp.int32)
         if g % 4 == 3:
             move(g // 4).start()
 
     fetch.start()
 
-    def add(g, _):
-        q, k = g >> 2, g & 3
-
-        @pl.when(k == 0)
-        def _():
-            move(q).wait()
-
-        lines = recv.at[pl.ds(pl.multiple_of(g * 8 * BLOCK, 8), 8 * BLOCK)]
-        for at in range(8 * SLOTS):
+    def add(q, _):
+        move(q).wait()
+        lines = recv.at[pl.ds(pl.multiple_of(q * 32 * BLOCK, 8), 32 * BLOCK)]
+        for at in range(32 * SLOTS):
             total = sums[at % CHAINS]
             line = at // SLOTS * BLOCK + at % SLOTS
-            spot = pl.ds(ids_s[q * 8 + k, at], 2, stride=PITCH)
+            spot = pl.ds(pl.multiple_of(ids_s[q * 8 + at // 128, at % 128], 2), 2)
             total[spot, :] = total[spot, :] + lines[pl.ds(line, 2, stride=SLOTS), :]
         return 0
 
-    lax.fori_loop(0, 16, add, 0)
+    lax.fori_loop(0, 4, add, 0)
 
     def fold(i, squared):
         squared = list(squared)
-        for k in range(8):
-            for j in range(2):
-                at = pl.multiple_of(j * PITCH + i * 64 + k * 8, 8)
-                parts = [total[pl.ds(at, 8), :] for total in sums]
-                while len(parts) > 1:
-                    parts = [sum(parts[k : k + 2]) for k in range(0, len(parts), 2)]
-                half[i * 8 + k, j] = parts[0]
-                squared[k % 4] = squared[k % 4] + parts[0] * parts[0]
+        for k in range(32):
+            at = pl.ds(pl.multiple_of(i * 256 + k * 8, 8), 8)
+            parts = [total[at, :] for total in sums]
+            while len(parts) > 1:
+                parts = [sum(parts[k : k + 2]) for k in range(0, len(parts), 2)]
+            half[at, :] = parts[0]
+            squared[k % 4] = squared[k % 4] + parts[0] * parts[0]
         return tuple(squared)
 
     zero = jnp.zeros((8, 128), jnp.float32)
-    a, b, c, d = lax.fori_loop(0, ROWS // 64, fold, (zero,) * 4)
+    a, b, c, d = lax.fori_loop(0, ROWS // 128, fold, (zero,) * 4)
     squares[...] = jnp.broadcast_to(jnp.sum((a + b) + (c + d), axis=0, keepdims=True), squares.shape)
     fetch.wait()
 
@@ -178,7 +172,7 @@
     return pl.pallas_call(
         sum_kernel,
         out_shape=(
-            jax.ShapeDtypeStruct((ROWS // 8, 2, 8, 128), jnp.float32),
+            jax.ShapeDtypeStruct((2 * ROWS, 128), jnp.float32),
             jax.ShapeDtypeStruct((DEVICES, 128), jnp.float32),
             jax.ShapeDtypeStruct((ROWS // 8, 4, 8, 128), jnp.float32),
         )
@@ -215,10 +209,10 @@
             cols = pl.ds(jnp.where(rep == 0, h, 1 - h) * 2, 2)
             ins = [ref.at[rows, cols] for ref in (table, moment, second)]
             to = [ref.at[rows, cols] for ref in bufs]
-            grads = source.at[rows]
+            grads = source.at[pl.ds(pl.multiple_of(i * 64, 64), 64)]
             for k in range(4):
                 for j in range(2):
-                    g = grads[k, j]
+                    g = grads[pl.ds(k * 16 + j, 8, stride=2), :]
                     nm = 0.9 * ins[1][k, j] + to_moment * g
                     nv = 0.999 * ins[2][k, j] + to_second * (g * g)
                     root = (nv * lax.rsqrt(nv)) * (1.0 / second_fix) ** 0.5 + 1e-08

time: 67.7 us -> 67.4 us (level)
  no operation moved by 1% of the time
where the time goes in v4:
time: 67.4 us; the launch traced here: 67.3 us
  blocking collectives  54.6 us (81%)
  Pallas kernels  10.6 us (16%)
  starting transfers between devices  1.46 us (2%)
    all_to_all x1, blocking collectives, local(): lax.all_to_all(send.reshape(DEVICES, 1, BLOCK * 128), AXES, 0, 0, tiled=T...  42.1 us
    all_to_all x1, blocking collectives, local(): lax.all_to_all(squares.reshape(DEVICES, 1, 128), AXES, 0, 0, tiled=True)  12.5 us
    pallas_call x1, Pallas kernels, update(): pl.pallas_call(update_kernel, out_shape=(shape,) * 3, in_specs=[pl.BlockS...  5.06 us
    pallas_call x1, Pallas kernels, sum_rows(): pl.pallas_call(sum_kernel, out_shape=(jax.ShapeDtypeStruct((2 * ROWS, 128...  3.23 us
    pallas_call x1, Pallas kernels, pack(): pl.pallas_call(pack_kernel, out_shape=(jax.ShapeDtypeStruct((DEVICES * BL...  2.28 us
    ppermute x1, starting transfers between devices, local(): other = lax.ppermute(half, 'rep', [(0, 1), (1, 0)])  1.46 us
  transfers between devices with their start and end apart: 1, of which 0 were waited for; matrix products, arithmetic and copies ran while one was open for 0% of the time, Pallas kernels for 0%

profile of v4, /device:TPU:1, one launch (start us, length us, event | category | flops | bytes accessed | tf_op | source)
XLA Modules:
  0.0 67.3 jit_solution(4131582179099239143)
XLA Ops:
  0.6 2.3 %pack.1 = (f32[4224,128]{1,0:T(8,128)S(1)}, f32[4128,128]{1,0:T(8,128)S(1)}, f32[4128,128]{1,0:T(8,128)S(1)}, f32[4128,128]{1,0:T(8,128)S(1)}, f32[4128,128]{1,0...) custom-call(s32[4,128]{1,0:T(4,128)} %bitcast.39, s32[4,128]{1,0:T(4,128)} %bitcast.40, f32[2048,128]{1,0:T(8,128)} %bitcast.38), custom_call_target="tpu_custom_call" | custom-call | tf_op jit(solution)/shard_map/pack/pallas_call | solution.py:104
  2.9 42.1 %all_to_all.10 = f32[128,1,4224]{2,1,0:T(1,128)S(1)} all-to-all(f32[128,1,4224]{2,1,0:T(1,128)S(1)} %bitcast.34), channel_id=1, replica_groups=mesh['dp'=64,'rep'=2] {'dp','rep'}, dimensions={0} | all-to-all | bytes 4325376 | tf_op jit(solution)/shard_map/all_to_all | solution.py:267
  45.0 0.0 copy-start
  45.0 0.0 copy-start.1
  45.0 3.2 %sum_rows.1 = (f32[4096,128]{1,0:T(8,128)S(1)}, f32[128,128]{1,0:T(8,128)S(1)}, f32[256,4,8,128]{3,2,1,0:T(8,128)S(1)}, f32[4128,128]{1,0:T(8,128)S(1)}, f32[412...) custom-call(f32[4224,128]{1,0:T(8,128)S(1)} %bitcast.31, ...), custom_call_target="tpu_custom_call", output_to_operand_aliasing={{3}: (2, {}), {4}: (3, {}), {5}: (4, {}), {6}: (5, {}), {7}... | custom-call | tf_op jit(solution)/shard_map/sum_rows/pallas_call | solution.py:172
  48.2 1.5 %collective-permute-start = (f32[4096,128]{1,0:T(8,128)S(1)}, f32[4096,128]{1,0:T(8,128)S(1)}, u32[]{:S(2)}, u32[]{:S(2)}) collective-permute-start(f32[4096,128]{1,0:T(8,128)S(1)} %get-tuple-element.24.own), channel_id=1, source_target_pairs={{0,1},{1,0},{2,3},{3,2},{4,5},{5,4},{6,7},{7,6},{8,9},{9,8},{10,11... | collective-permute-start | bytes 6291464 | tf_op jit(solution)/shard_map/ppermute | solution.py:271
  49.7 12.5 %all_to_all.11 = f32[128,1,128]{2,1,0:T(1,128)S(1)} all-to-all(f32[128,1,128]{2,1,0:T(1,128)S(1)} %bitcast.36), channel_id=1, replica_groups=mesh['dp'=64,'rep'=2] {'dp','rep'}, dimensions={0} | all-to-all | bytes 131072 | tf_op jit(solution)/shard_map/all_to_all | solution.py:270
  62.2 0.0 collective-permute-done.other
  62.2 0.0 copy-done
  62.2 0.0 copy-done.1
  62.2 5.1 %update.1 = (f32[256,4,8,128]{3,2,1,0:T(8,128)}, f32[256,4,8,128]{3,2,1,0:T(8,128)}, f32[256,4,8,128]{3,2,1,0:T(8,128)}) custom-call(f32[128,128]{1,0:T(8,128)S(1)} %bitcast.35, f32[4096,128]{1,0:T(8,128)S(1)} %get-tuple-element.24.own, f32[4096,128]{1,0:T(8,128)S(1)} %collective-permute-done.other, f32[256,4,8,128]{3,2,1,0:T(8,128)S(1)} %bitcast.32, ...), custom_call_target="tpu_custom_call" | custom-call | tf_op jit(solution)/shard_map/update/pallas_call | solution.py:247
Async XLA Ops:
  45.0 17.2 %copy-start = (f32[2048,512]{1,0:T(8,128)S(1)}, f32[2048,512]{1,0:T(8,128)}, u32[]{:S(2)}) copy-start(f32[2048,512]{1,0:T(8,128)} %param.9) | copy-start | bytes 12582916
  45.0 17.2 %copy-start.1 = (f32[2048,512]{1,0:T(8,128)S(1)}, f32[2048,512]{1,0:T(8,128)}, u32[]{:S(2)}) copy-start(f32[2048,512]{1,0:T(8,128)} %param.10) | copy-start | bytes 12582916
  48.2 14.0 %collective-permute-start = (f32[4096,128]{1,0:T(8,128)S(1)}, f32[4096,128]{1,0:T(8,128)S(1)}, u32[]{:S(2)}, u32[]{:S(2)}) collective-permute-start(f32[4096,128]{1,0:T(8,128)S(1)} %get-tuple-element.24.own), channel_id=1, source_target_pairs={{0,1},{1,0},{2,3},{3,2},{4,5},{5,4},{6,7},{7,6},{8,9},{9,8},{10,11... | collective-permute-start | bytes 6291464 | tf_op jit(solution)/shard_map/ppermute | solution.py:271

commit v5 on v4

--- a/solution.py
+++ b/solution.py
@@ -16,7 +16,7 @@
 BLOCK = 2 * SLOTS + 1
 PITCH = 2064
 CHAINS = 6
-CHUNKS = (8, 16, 24, 36, 52, 64, 56)
+CHUNKS = (12, 16, 20, 28, 36, 48, 60, 36)
 AXES = ("dp", "rep")
 VMEM = pltpu.MemorySpace.VMEM
 SMEM = pltpu.MemorySpace.SMEM
@@ -46,7 +46,7 @@
                 total[pl.ds(i * 32 + k * 8, 8), :] = jnp.zeros((8, 128), jnp.float32)
         return 0
 
-    lax.fori_loop(0, 2 * PITCH // 64, clear, 0)
+    lax.fori_loop(0, 86, clear, 0)
     loads[0].wait()
     masks = [who == owner_v[i : i + 1, :] for i in range(4)]
     hots = [jnp.where(mask, 1.0, 0.0).astype(jnp.bfloat16) for mask in masks]
@@ -84,7 +84,7 @@
         for h in range(2):
             spot = (16 * a + h) * BLOCK + 2 * SLOTS
             send[pl.ds(spot, 8, stride=2 * BLOCK), :] = ids[8 * a : 8 * a + 8]
-    lax.fori_loop(2 * PITCH // 64, 2 * PITCH // 32, clear, 0)
+    lax.fori_loop(86, 2 * PITCH // 32, clear, 0)
     loads[2].wait()
     move.wait()
 
@@ -120,11 +120,10 @@
     )(*(pltpu.with_memory_space_constraint(a, HBM) for a in (owner, row, x)))
 
 
-def sum_kernel(recv, second, *refs):
-    half, squares, second_v = refs[CHAINS : CHAINS + 3]
-    sums = refs[CHAINS + 3 : 2 * CHAINS + 3]
-    ids_v, ids_s, id_sems, sem = refs[2 * CHAINS + 3 :]
-    fetch = pltpu.make_async_copy(second, second_v, sem)
+def sum_kernel(recv, *refs):
+    half, squares = refs[CHAINS : CHAINS + 2]
+    sums = refs[CHAINS + 2 : 2 * CHAINS + 2]
+    ids_v, ids_s, id_sems = refs[2 * CHAINS + 2 :]
     def move(q):
         part = pl.ds(pl.multiple_of(q * 8, 8), 8)
         return pltpu.make_async_copy(ids_v.at[part], ids_s.at[part], id_sems.at[q])
@@ -136,7 +135,6 @@
         if g % 4 == 3:
             move(g // 4).start()
 
-    fetch.start()
 
     def add(q, _):
         move(q).wait()
@@ -164,32 +162,28 @@
     zero = jnp.zeros((8, 128), jnp.float32)
     a, b, c, d = lax.fori_loop(0, ROWS // 128, fold, (zero,) * 4)
     squares[...] = jnp.broadcast_to(jnp.sum((a + b) + (c + d), axis=0, keepdims=True), squares.shape)
-    fetch.wait()
-
-
-def sum_rows(recv, second, sums):
+
+
+def sum_rows(recv, sums):
     total = jax.ShapeDtypeStruct((2 * PITCH, 128), jnp.float32)
     return pl.pallas_call(
         sum_kernel,
         out_shape=(
             jax.ShapeDtypeStruct((2 * ROWS, 128), jnp.float32),
             jax.ShapeDtypeStruct((DEVICES, 128), jnp.float32),
-            jax.ShapeDtypeStruct((ROWS // 8, 4, 8, 128), jnp.float32),
         )
         + (total,) * CHAINS,
-        in_specs=[pl.BlockSpec(memory_space=VMEM), pl.BlockSpec(memory_space=HBM)]
-        + [pl.BlockSpec(memory_space=VMEM)] * CHAINS,
-        out_specs=(pl.BlockSpec(memory_space=VMEM),) * (3 + CHAINS),
+        in_specs=[pl.BlockSpec(memory_space=VMEM)] * (1 + CHAINS),
+        out_specs=(pl.BlockSpec(memory_space=VMEM),) * (2 + CHAINS),
         scratch_shapes=[
             pltpu.VMEM((32, 128), jnp.int32),
             pltpu.SMEM((32, 128), jnp.int32),
             pltpu.SemaphoreType.DMA((4,)),
-            pltpu.SemaphoreType.DMA,
         ],
-        input_output_aliases={2 + c: 3 + c for c in range(CHAINS)},
+        input_output_aliases={1 + c: 2 + c for c in range(CHAINS)},
         compiler_params=pltpu.CompilerParams(vmem_limit_bytes=22 * 2**20),
         name="sum_rows",
-    )(recv, pltpu.with_memory_space_constraint(second, HBM), *sums)
+    )(recv, *sums)
 
 
 def update_kernel(part, own, other, table, moment, second, *rest):
@@ -266,10 +260,10 @@
     send, *sums = pack(token_owner.reshape(4, 128), token_row.reshape(4, 128), x)
     recv = lax.all_to_all(send.reshape(DEVICES, 1, BLOCK * 128), AXES, 0, 0, tiled=True)
     lines = recv.reshape(DEVICES * BLOCK, 128)
-    half, squares, second = sum_rows(lines, tiles(second), sums)[:3]
+    half, squares = sum_rows(lines, sums)[:2]
     part = lax.all_to_all(squares.reshape(DEVICES, 1, 128), AXES, 0, 0, tiled=True)
     other = lax.ppermute(half, "rep", [(0, 1), (1, 0)])
-    outs = update(part.reshape(DEVICES, 128), half, other, tiles(table), tiles(moment), second)
+    outs = update(part.reshape(DEVICES, 128), half, other, tiles(table), tiles(moment), tiles(second))
     return tuple(out.transpose(0, 2, 1, 3).reshape(ROWS, LW) for out in outs)
 
 

time: 67.4 us -> 67.2 us (level)
  no operation moved by 1% of the time
where the time goes in v5:
time: 67.2 us; the launch traced here: 67.1 us
  blocking collectives  54.6 us (81%)
  Pallas kernels  10.4 us (15%)
  starting transfers between devices  1.46 us (2%)
    all_to_all x1, blocking collectives, local(): lax.all_to_all(send.reshape(DEVICES, 1, BLOCK * 128), AXES, 0, 0, tiled=T...  42.1 us
    all_to_all x1, blocking collectives, local(): lax.all_to_all(squares.reshape(DEVICES, 1, 128), AXES, 0, 0, tiled=True)  12.5 us
    pallas_call x1, Pallas kernels, update(): pl.pallas_call(update_kernel, out_shape=(shape,) * 3, in_specs=[pl.BlockS...  5.04 us
    pallas_call x1, Pallas kernels, sum_rows(): pl.pallas_call(sum_kernel, out_shape=(jax.ShapeDtypeStruct((2 * ROWS, 128...  3.28 us
    pallas_call x1, Pallas kernels, pack(): pl.pallas_call(pack_kernel, out_shape=(jax.ShapeDtypeStruct((DEVICES * BL...  2.12 us
    ppermute x1, starting transfers between devices, local(): other = lax.ppermute(half, 'rep', [(0, 1), (1, 0)])  1.46 us
  transfers between devices with their start and end apart: 1, of which 0 were waited for; matrix products, arithmetic and copies ran while one was open for 0% of the time, Pallas kernels for 0%

profile of v5, /device:TPU:1, one launch (start us, length us, event | category | flops | bytes accessed | tf_op | source)
XLA Modules:
  0.0 67.1 jit_solution(8791831081899056297)
XLA Ops:
  0.6 2.1 %pack.1 = (f32[4224,128]{1,0:T(8,128)S(1)}, f32[4128,128]{1,0:T(8,128)S(1)}, f32[4128,128]{1,0:T(8,128)S(1)}, f32[4128,128]{1,0:T(8,128)S(1)}, f32[4128,128]{1,0...) custom-call(s32[4,128]{1,0:T(4,128)} %bitcast.39, s32[4,128]{1,0:T(4,128)} %bitcast.40, f32[2048,128]{1,0:T(8,128)} %bitcast.38), custom_call_target="tpu_custom_call" | custom-call | tf_op jit(solution)/shard_map/pack/pallas_call | solution.py:104
  2.8 42.1 %all_to_all.10 = f32[128,1,4224]{2,1,0:T(1,128)S(1)} all-to-all(f32[128,1,4224]{2,1,0:T(1,128)S(1)} %bitcast.35), channel_id=1, replica_groups=mesh['dp'=64,'rep'=2] {'dp','rep'}, dimensions={0} | all-to-all | bytes 4325376 | tf_op jit(solution)/shard_map/all_to_all | solution.py:261
  44.8 0.0 copy-start
  44.8 0.0 copy-start.1
  44.8 0.0 copy-start.2
  44.8 3.3 %sum_rows.1 = (f32[4096,128]{1,0:T(8,128)S(1)}, f32[128,128]{1,0:T(8,128)S(1)}, f32[4128,128]{1,0:T(8,128)S(1)}, f32[4128,128]{1,0:T(8,128)S(1)}, f32[4128,128]{...) custom-call(f32[4224,128]{1,0:T(8,128)S(1)} %bitcast.31, ...), custom_call_target="tpu_custom_call", output_to_operand_aliasing={{2}: (1, {}), {3}: (2, {}), {4}: (3, {}), {5}: (4, {}), {6}... | custom-call | tf_op jit(solution)/shard_map/sum_rows/pallas_call | solution.py:169
  48.1 1.5 %collective-permute-start = (f32[4096,128]{1,0:T(8,128)S(1)}, f32[4096,128]{1,0:T(8,128)S(1)}, u32[]{:S(2)}, u32[]{:S(2)}) collective-permute-start(f32[4096,128]{1,0:T(8,128)S(1)} %get-tuple-element.23.own), channel_id=1, source_target_pairs={{0,1},{1,0},{2,3},{3,2},{4,5},{5,4},{6,7},{7,6},{8,9},{9,8},{10,11... | collective-permute-start | bytes 6291464 | tf_op jit(solution)/shard_map/ppermute | solution.py:265
  49.6 12.5 %all_to_all.11 = f32[128,1,128]{2,1,0:T(1,128)S(1)} all-to-all(f32[128,1,128]{2,1,0:T(1,128)S(1)} %bitcast.37), channel_id=1, replica_groups=mesh['dp'=64,'rep'=2] {'dp','rep'}, dimensions={0} | all-to-all | bytes 131072 | tf_op jit(solution)/shard_map/all_to_all | solution.py:264
  62.1 0.0 collective-permute-done.other
  62.1 0.0 copy-done
  62.1 0.0 copy-done.1
  62.1 0.0 copy-done.2
  62.1 5.0 %update.1 = (f32[256,4,8,128]{3,2,1,0:T(8,128)}, f32[256,4,8,128]{3,2,1,0:T(8,128)}, f32[256,4,8,128]{3,2,1,0:T(8,128)}) custom-call(f32[128,128]{1,0:T(8,128)S(1)} %bitcast.36, f32[4096,128]{1,0:T(8,128)S(1)} %get-tuple-element.23.own, f32[4096,128]{1,0:T(8,128)S(1)} %collective-permute-done.other, f32[256,4,8,128]{3,2,1,0:T(8,128)S(1)} %bitcast.32, ...), custom_call_target="tpu_custom_call" | custom-call | tf_op jit(solution)/shard_map/update/pallas_call | solution.py:241
Async XLA Ops:
  44.8 17.2 %copy-start = (f32[2048,512]{1,0:T(8,128)S(1)}, f32[2048,512]{1,0:T(8,128)}, u32[]{:S(2)}) copy-start(f32[2048,512]{1,0:T(8,128)} %param.9) | copy-start | bytes 12582916
  44.8 17.2 %copy-start.1 = (f32[2048,512]{1,0:T(8,128)S(1)}, f32[2048,512]{1,0:T(8,128)}, u32[]{:S(2)}) copy-start(f32[2048,512]{1,0:T(8,128)} %param.10) | copy-start | bytes 12582916
  44.8 17.2 %copy-start.2 = (f32[2048,512]{1,0:T(8,128)S(1)}, f32[2048,512]{1,0:T(8,128)}, u32[]{:S(2)}) copy-start(f32[2048,512]{1,0:T(8,128)} %param.11) | copy-start | bytes 12582916
  48.1 14.0 %collective-permute-start = (f32[4096,128]{1,0:T(8,128)S(1)}, f32[4096,128]{1,0:T(8,128)S(1)}, u32[]{:S(2)}, u32[]{:S(2)}) collective-permute-start(f32[4096,128]{1,0:T(8,128)S(1)} %get-tuple-element.23.own), channel_id=1, source_target_pairs={{0,1},{1,0},{2,3},{3,2},{4,5},{5,4},{6,7},{7,6},{8,9},{9,8},{10,11... | collective-permute-start | bytes 6291464 | tf_op jit(solution)/shard_map/ppermute | solution.py:265
